TPU v7x, 32 devices: a whole 2x2x4 slice. The times are simulated.
32 devices in a mesh: seg: 4 (over z), cp: 8 (over y, x, core).
Axes of the slice: x: 2, y: 2, z: 4, core: 2. Of those that a mesh axis runs over, the one named last changes fastest.
Arguments:
- mixed_qkv: bfloat16 [4096, 8192], P(('seg', 'cp')), may hold values from -6 to 6
- gate_z: bfloat16 [4096, 4096], P(('seg', 'cp')), may hold values from -6 to 6
- gate_logits: bfloat16 [4096, 64], P(('seg', 'cp')), may hold values from -16 to 4
- block_table: int32 [4, 16], P('seg'), may hold values from 0 to 15, as said below
- conv_weight: float32 [4, 8192], replicated, may hold values from -3 to 3
- a_log: float32 [32], replicated, may hold values from -0.7 to 0.7
- dt_bias: float32 [32], replicated, may hold values from -0.5 to 0.5
- norm_gain: float32 [128], replicated, may hold values from 0.25 to 1.75
Outputs:
- mixed_out: bfloat16 [4096, 4096], P(('seg', 'cp'))
Inputs may be any that keep to these rules, and one draw needn't show every extreme that they name: Each row of block_table is a permutation of the numbers 0 to 15; its entries at even positions are below 8, those at odd positions are 8 or more.
All inputs are finite; a program needn't handle non-finite values.
Results may differ from a plain program's by a relative error of at most 0.001.
Values may be sent and summed in bfloat16 or wider, within the bound.
A program may use at most 128 MiB of HBM per device.

v0:
```python
import functools

import jax
import jax.numpy as jnp
from jax import lax
from jax.experimental import pallas as pl
from jax.experimental.pallas import tpu as pltpu
from jax.sharding import PartitionSpec as P

VALUE_HEADS = 32
KEY_HEADS = 16
HEAD_DIM = 128
CONV = 4
BLOCK = 128
TAIL = 8
GROUP = VALUE_HEADS // KEY_HEADS
PAIR = 2

f32 = jnp.float32
bf16 = jnp.bfloat16
MESH = pl.DeviceIdType.MESH
highest = lax.Precision.HIGHEST


def split(x):
    hi = x.astype(bf16)
    return hi, (x - hi.astype(f32)).astype(bf16)


NN = (((1,), (0,)), ((), ()))
NT = (((1,), (1,)), ((), ()))


def mm(a, b, dims=NN):
    def dot(x, y):
        return lax.dot_general(x, y, dims, preferred_element_type=f32)

    if dims == NT:
        return dot(a[0], b[0]) + (dot(a[0], b[1]) + dot(a[1], b[0]))
    wide = jnp.concatenate(a, axis=1)
    if b[0].shape[1] > HEAD_DIM:
        return dot(wide, jnp.concatenate([b[0], b[0]], axis=0)) + dot(a[0], b[1])
    top = jnp.concatenate([b[0], b[1]], axis=1)
    low = jnp.concatenate([b[0], jnp.zeros_like(b[1])], axis=1)
    both = dot(wide, jnp.concatenate([top, low], axis=0))
    return both[:, :HEAD_DIM] + both[:, HEAD_DIM:]


def log1p_exact(y):
    u = 1.0 + y
    return jnp.where(u == 1.0, y, jnp.log(u) * (y / jnp.where(u == 1.0, 1.0, u - 1.0)))


def prepare(
    heads, b, start, order, parts_now, first_prior, head_start, w_ref, rate_ref, x_ref
):
    keys = max(1, heads // GROUP)
    wk, wv = keys * HEAD_DIM, heads * HEAD_DIM
    i0 = order[2 * b] // 2
    i1 = order[2 * b + 1] // 2
    ip = order[jnp.maximum(2 * b - 1, 0)] // 2
    half = parts_now[0].shape[1]

    row = lax.broadcasted_iota(jnp.int32, (BLOCK, BLOCK), 0)
    col = lax.broadcasted_iota(jnp.int32, (BLOCK, BLOCK), 1)
    strict = row > col
    inclusive = row >= col
    eye = jnp.where(row == col, 1.0, 0.0).astype(f32)

    at = 0
    for place, width in enumerate((wk, wk, wv)):
        cols = slice(at, at + width)
        ref = parts_now[place]
        prior = ref[ip, half - 16 :, :].astype(f32)[8:]
        x_ref[0:8, cols] = jnp.where(b == start, first_prior(place, cols), prior)
        x_ref[8 : 8 + half, cols] = ref[i0].astype(f32)
        x_ref[8 + half : 8 + 2 * half, cols] = ref[i1].astype(f32)
        at += width

    def conv(start):
        cols = slice(start, start + HEAD_DIM)
        total_rows = w_ref[0:1, cols] * x_ref[5 : 5 + BLOCK, cols]
        for j in range(1, CONV):
            total_rows = total_rows + w_ref[j : j + 1, cols] * x_ref[5 + j : 5 + j + BLOCK, cols]
        return total_rows / (1.0 + jnp.exp(-total_rows))

    def unit(x):
        return x * lax.rsqrt(jnp.sum(x * x, axis=-1, keepdims=True) + 1e-06)

    gates = jnp.concatenate([parts_now[3][i0], parts_now[3][i1]], axis=0).astype(f32)
    gates = jnp.concatenate([gates, jnp.zeros((BLOCK, BLOCK - gates.shape[1]), f32)], axis=1)
    beta_all = 1.0 / (1.0 + jnp.exp(-gates))
    shifted = gates + rate_ref[1:2, :]
    soft = jnp.maximum(shifted, 0.0) + log1p_exact(jnp.exp(-jnp.abs(shifted)))
    decays = rate_ref[0:1, :] * soft
    turn = lax.rem(BLOCK - head_start, BLOCK)
    beta_all = pltpu.roll(beta_all, turn, 1)
    decays = pltpu.roll(decays, turn, 1)
    tril = jnp.where(inclusive, 1.0, 0.0).astype(bf16)
    d0 = decays.astype(bf16)
    rest = decays - d0.astype(f32)
    d1 = rest.astype(bf16)
    d2 = (rest - d1.astype(f32)).astype(bf16)
    cum = jnp.dot(tril, d2, preferred_element_type=f32)
    cum = cum + jnp.dot(tril, d1, preferred_element_type=f32)
    cum = cum + jnp.dot(tril, d0, preferred_element_type=f32)
    cum_t = jnp.transpose(cum)

    queries, key_rows, kk, qk = [], [], [], []
    for g in range(keys):
        queries.append(unit(conv(g * HEAD_DIM)) * HEAD_DIM ** (-0.5))
        key_rows.append(unit(conv(wk + g * HEAD_DIM)))
        ks = split(key_rows[g])
        qs = split(queries[g])
        kk.append(mm(ks, ks, NT))
        qk.append(mm(qs, ks, NT))

    hs = range(heads)
    lower, scores, rhs, kdt, qd, last = [], [], [], [], [], []
    for h in hs:
        g = h * keys // heads
        beta = beta_all[:, h : h + 1]
        c = cum[:, VALUE_HEADS + h : VALUE_HEADS + h + 1]
        ct = cum_t[VALUE_HEADS + h : VALUE_HEADS + h + 1, :]
        final = ct[:, BLOCK - 1 :]
        spread = c - ct
        incl = jnp.where(inclusive, jnp.exp(jnp.where(inclusive, spread, 0.0)), 0.0)
        lower.append(jnp.where(strict, beta * kk[g] * incl, 0.0))
        scores.append(split(qk[g] * incl))
        grow = jnp.exp(c)
        values = conv(2 * wk + h * HEAD_DIM)
        rhs.append(split(jnp.concatenate([values * beta, key_rows[g] * (beta * grow)], axis=1)))
        kdt.append(split(jnp.transpose(key_rows[g] * jnp.exp(final - c))))
        qd.append(queries[g] * grow)
        last.append(jnp.exp(final))

    return lower, scores, rhs, kdt, qd, last


def block_pair(
    heads, pair, start, order, parts_now, first_prior, head_start, w_ref, rate_ref, o_ref, mh_ref, ml_ref, st_ref, x_ref
):
    row = lax.broadcasted_iota(jnp.int32, (BLOCK, BLOCK), 0)
    col = lax.broadcasted_iota(jnp.int32, (BLOCK, BLOCK), 1)
    eye = jnp.where(row == col, 1.0, 0.0).astype(f32)
    lower, scores, rhs, kdt, qd, last = [], [], [], [], [], []
    for e in range(PAIR):
        found = prepare(
            heads, PAIR * pair + e, start, order, parts_now, first_prior, head_start, w_ref, rate_ref, x_ref.at[e]
        )
        for total, more in zip((lower, scores, rhs, kdt, qd, last), found):
            total += more
    hs = range(PAIR * heads)

    def same(size):
        return (row // size) == (col // size)

    small = 16
    power = [split(jnp.where(same(small), -lower[h], 0.0)) for h in hs]
    inverse = [eye + jnp.where(same(small), -lower[h], 0.0) for h in hs]
    steps = 1
    while 2**steps < small:
        power = [split(mm(power[h], power[h])) for h in hs]
        inverse = [inverse[h] + mm(split(inverse[h]), power[h]) for h in hs]
        steps += 1
    size = small
    while size < BLOCK:
        between = same(2 * size) & (~same(size))
        cross = [split(jnp.where(between, lower[h], 0.0)) for h in hs]
        parts = [split(inverse[h]) for h in hs]
        mixed = [split(mm(cross[h], parts[h])) for h in hs]
        inverse = [inverse[h] - mm(parts[h], mixed[h]) for h in hs]
        size *= 2
    solved = [split(mm(split(inverse[h]), rhs[h])) for h in hs]
    outs = [mm(scores[h], solved[h]) for h in hs]
    ends = [mm(kdt[h], solved[h]) for h in hs]
    readers = [split(qd[h] - outs[h][:, HEAD_DIM:]) for h in hs]
    maps = [split(last[h] * eye - ends[h][:, HEAD_DIM:]) for h in hs]
    for e in range(PAIR):
        b = PAIR * pair + e
        states = [split(st_ref[h]) for h in range(heads)]
        for h in range(heads):
            at = e * heads + h
            moved = mm(maps[at], states[h])
            st_ref[h] = jnp.concatenate(
                [moved[:, :HEAD_DIM] + ends[at][:, :HEAD_DIM], moved[:, HEAD_DIM:]], axis=1
            )
        for h in range(heads):
            at = e * heads + h
            seen = mm(readers[at], states[h])
            o_ref[h, b] = seen[:, :HEAD_DIM] + outs[at][:, :HEAD_DIM]
            reach = split(seen[:, HEAD_DIM:])
            mh_ref[h, b] = reach[0]
            ml_ref[h, b] = reach[1]


def mix_kernel(
    n, segs, heads, order, qkv, z, gates, conv_weight, rate_ref, o_ref, mh_ref, ml_ref, st_ref, oz,
    qa, ka, va, ga, qb, kb, vb, gb, otail, w_ref, x_ref, send, recv, local
):
    me = lax.axis_index("cp")
    seg = lax.axis_index("seg")
    after = lax.rem(seg + 1, segs)
    before = lax.rem(seg + segs - 1, segs)
    keys = max(1, heads // GROUP)
    wk, wv = keys * HEAD_DIM, heads * HEAD_DIM
    key_width = KEY_HEADS * HEAD_DIM
    rows = qkv.shape[0]
    half = rows // 2

    barrier = pltpu.get_barrier_semaphore()
    for d in range(n):
        peer = lax.rem(me + d, n)
        if d:
            pl.semaphore_signal(barrier, inc=1, device_id=(seg, peer), device_id_type=MESH)
        pl.semaphore_signal(barrier, inc=1, device_id=(before, peer), device_id_type=MESH)

    def columns(start, width):
        return pl.ds(pl.multiple_of(start, HEAD_DIM), width)

    def pieces(p, slot):
        kcol = lax.div(p * heads, GROUP) * HEAD_DIM
        vcol = p * wv
        found = []
        for first, bufs in ((0, (qa, ka, va, ga)), (half, (qb, kb, vb, gb))):
            these = pl.ds(first, half)
            found += [
                (qkv.at[these, columns(kcol, wk)], bufs[0].at[slot]),
                (qkv.at[these, columns(key_width + kcol, wk)], bufs[1].at[slot]),
                (qkv.at[these, columns(2 * key_width + vcol, wv)], bufs[2].at[slot]),
                (gates.at[these], bufs[3].at[slot]),
            ]
        return found + [
            (z.at[pl.ds(0, half), columns(vcol, wv)], oz.at[2 * slot]),
            (z.at[pl.ds(half, half), columns(vcol, wv)], oz.at[2 * slot + 1]),
        ]

    def tails(p, slot):
        kcol = lax.div(p * heads, GROUP) * HEAD_DIM
        vcol = p * wv
        last = pl.ds(rows - TAIL, TAIL)
        return [
            (qkv.at[last, columns(kcol, wk)], otail.at[slot, :, pl.ds(0, wk)]),
            (qkv.at[last, columns(key_width + kcol, wk)], otail.at[slot, :, pl.ds(wk, wk)]),
            (qkv.at[last, columns(2 * key_width + vcol, wv)], otail.at[slot, :, pl.ds(2 * wk, wv)]),
        ]

    own = []
    kcol = lax.div(me * heads, GROUP) * HEAD_DIM
    mine = pieces(me, me) + [
        (conv_weight.at[:, columns(kcol, wk)], w_ref.at[:, pl.ds(0, wk)]),
        (conv_weight.at[:, columns(key_width + kcol, wk)], w_ref.at[:, pl.ds(wk, wk)]),
        (conv_weight.at[:, columns(2 * key_width + me * wv, wv)], w_ref.at[:, pl.ds(2 * wk, wv)]),
    ]
    for kind, (src, dst) in enumerate(mine):
        copy = pltpu.make_async_copy(src, dst, local.at[kind])
        copy.start()
        own.append(copy)
    pl.semaphore_wait(barrier, 2 * n - 1)

    started = []

    def post(kind, src, dst, peer, target):
        copy = pltpu.make_async_remote_copy(
            src_ref=src,
            dst_ref=dst,
            send_sem=send.at[kind, peer],
            recv_sem=recv.at[kind, me],
            device_id=target,
            device_id_type=MESH,
        )
        copy.start()
        started.append(copy)

    for kinds in ((0, 1, 2, 3), (4, 5, 6, 7), (8, 9)):
        for d in range(1, n):
            peer = lax.rem(me + d, n)
            sources = pieces(peer, me)
            for kind in kinds:
                post(kind, *sources[kind], peer, (seg, peer))
        if kinds[0] == 0:
            for d in range(n):
                peer = lax.rem(me + d, n)
                for i, (src, dst) in enumerate(tails(peer, me)):
                    post(10 + i, src, dst, peer, (after, peer))

    def arrived(kinds):
        for d in range(n):
            source = lax.rem(me + n - d, n)
            found = pieces(me, source) + tails(me, source)
            for kind in kinds:
                if d or kind > 9:
                    src, dst = found[kind]
                    pltpu.make_async_remote_copy(
                        src_ref=src,
                        dst_ref=dst,
                        send_sem=send.at[kind, source],
                        recv_sem=recv.at[kind, source],
                        device_id=(seg, source),
                        device_id_type=MESH,
                    ).wait_recv()

    row = lax.broadcasted_iota(jnp.int32, (HEAD_DIM, HEAD_DIM), 0)
    col = lax.broadcasted_iota(jnp.int32, (HEAD_DIM, HEAD_DIM), 1)
    for h in range(heads):
        st_ref[h, :, :HEAD_DIM] = jnp.zeros((HEAD_DIM, HEAD_DIM), f32)
        st_ref[h, :, HEAD_DIM:] = jnp.where(row == col, 1.0, 0.0).astype(f32)
    for copy in own:
        copy.wait()
    tail_from = order[2 * n]
    joint = order[n - 1] // 2
    early = (qa, ka, va, ga)
    late = (qb, kb, vb, gb)

    def from_tail(place, cols):
        return jnp.where(seg == 0, 0.0, otail[tail_from].astype(f32)[:, cols])

    def from_early(place, cols):
        return early[place][joint, half - 16 :, :].astype(f32)[8:]

    def run(first, stop, bufs, prior):
        def one(b, carry):
            block_pair(
                heads, b, first, order, bufs, prior, me * heads,
                w_ref, rate_ref, o_ref, mh_ref, ml_ref, st_ref, x_ref,
            )
            return carry

        lax.fori_loop(first // PAIR, stop // PAIR, one, 0)

    arrived((0, 1, 2, 3, 10, 11, 12))
    run(0, n // 2, early, from_tail)
    arrived((4, 5, 6, 7))
    run(n // 2, n, late, from_early)
    arrived((8, 9))
    for copy in started:
        copy.wait_send()


def close_kernel(
    n, segs, heads, order, end_ref, o_ref, mh_ref, ml_ref, z_ref, gain_ref, out,
    inc_ref, pass_ref, y_ref, send, recv, ysend, yrecv, local
):
    seg = lax.axis_index("seg")
    me = lax.axis_index("cp")
    final = segs - 1
    width = heads * HEAD_DIM
    def hop(h):
        return pltpu.make_async_remote_copy(
            src_ref=pass_ref.at[h],
            dst_ref=inc_ref.at[h],
            send_sem=send.at[h],
            recv_sem=recv.at[h],
            device_id=(lax.rem(seg + 1, segs), me),
            device_id_type=MESH,
        )

    @pl.when(seg == 0)
    def _():
        for h in range(heads):
            inc_ref[h] = jnp.zeros((HEAD_DIM, HEAD_DIM), f32)
            pass_ref[h] = end_ref[h, :, :HEAD_DIM]
        for h in range(heads):
            hop(h).start()

    @pl.when((seg > 0) & (seg < final))
    def _():
        for h in range(heads):
            through = split(end_ref[h, :, HEAD_DIM:])
            hop(h).wait_recv()
            pass_ref[h] = end_ref[h, :, :HEAD_DIM] + mm(through, split(inc_ref[h]))
            hop(h).start()

    def block(h, b, state):
        cols = pl.ds(h * HEAD_DIM, HEAD_DIM)
        i0 = order[2 * b]
        i1 = order[2 * b + 1]
        core = o_ref[h, b] + mm((mh_ref[h, b], ml_ref[h, b]), state)
        z = jnp.concatenate([z_ref[i0, :, cols], z_ref[i1, :, cols]], axis=0).astype(f32)
        scale = lax.rsqrt(jnp.sum(core * core, axis=-1, keepdims=True) * (1.0 / HEAD_DIM) + 1e-06)
        y_ref[h, b] = (core * scale * gain_ref[0:1, :] * (z / (1.0 + jnp.exp(-z)))).astype(bf16)

    def target(h, source):
        return out.at[:, pl.ds(pl.multiple_of(source * width + h * HEAD_DIM, HEAD_DIM), HEAD_DIM)]

    def give(h, d):
        peer = lax.rem(me + d, n)
        return pltpu.make_async_remote_copy(
            src_ref=y_ref.at[h, peer],
            dst_ref=target(h, me),
            send_sem=ysend.at[h, peer],
            recv_sem=yrecv.at[h, me],
            device_id=(seg, peer),
            device_id_type=MESH,
        )

    for h in range(heads):
        @pl.when(seg == final)
        def _():
            hop(h).wait_recv()

        state = split(inc_ref[h])

        for d in range(1, n):
            block(h, lax.rem(me + d, n), state)
            if d > 1:
                give(h, d - 1).start()
        block(h, me, state)
        give(h, n - 1).start()
        if h:
            pltpu.make_async_copy(y_ref.at[h - 1, me], target(h - 1, me), local.at[h - 1]).start()
    pltpu.make_async_copy(y_ref.at[heads - 1, me], target(heads - 1, me), local.at[heads - 1]).start()

    for h in range(heads):
        pltpu.make_async_copy(y_ref.at[h, me], target(h, me), local.at[h]).wait()
        for d in range(1, n):
            source = lax.rem(me + n - d, n)
            pltpu.make_async_remote_copy(
                src_ref=y_ref.at[h, source],
                dst_ref=target(h, source),
                send_sem=ysend.at[h, source],
                recv_sem=yrecv.at[h, source],
                device_id=(seg, source),
                device_id_type=MESH,
            ).wait_recv()
    for h in range(heads):
        for d in range(1, n):
            give(h, d).wait_send()

        @pl.when(seg < final)
        def _():
            hop(h).wait_send()


def whole_kernel(
    n, segs, heads, order, qkv, z, gates, conv_weight, rate_ref, gain_ref, out,
    o_ref, mh_ref, ml_ref, st_ref, oz, inc_ref, pass_ref, y_ref, *rest
):
    bufs, sems = rest[:11], rest[11:]
    mix_kernel(
        n, segs, heads, order, qkv, z, gates, conv_weight, rate_ref,
        o_ref, mh_ref, ml_ref, st_ref, oz, *bufs, *sems[:3],
    )
    close_kernel(
        n, segs, heads, order, st_ref, o_ref, mh_ref, ml_ref, oz, gain_ref, out,
        inc_ref, pass_ref, y_ref, *sems[3:],
    )


def mixer(n, segs, heads, order, qkv, z, gates, conv_weight, rates, gain):
    keys = max(1, heads // GROUP)
    wk, wv = keys * HEAD_DIM, heads * HEAD_DIM
    half = qkv.shape[0] // 2
    anywhere = pl.BlockSpec(memory_space=pl.ANY)
    vmem = pl.BlockSpec(memory_space=pltpu.VMEM)
    widths = (wk, wk, wv, gates.shape[1])
    square = (HEAD_DIM, HEAD_DIM)
    DMA = pltpu.SemaphoreType.DMA
    return pl.pallas_call(
        functools.partial(whole_kernel, n, segs, heads),
        out_shape=jax.ShapeDtypeStruct((BLOCK, n * heads * HEAD_DIM), bf16),
        in_specs=[pl.BlockSpec(memory_space=pltpu.SMEM)] + [anywhere] * 4 + [vmem] * 2,
        out_specs=vmem,
        scratch_shapes=[
            pltpu.VMEM((heads, n, BLOCK, HEAD_DIM), f32),
            pltpu.VMEM((heads, n, BLOCK, HEAD_DIM), bf16),
            pltpu.VMEM((heads, n, BLOCK, HEAD_DIM), bf16),
            pltpu.VMEM((heads, HEAD_DIM, 2 * HEAD_DIM), f32),
            pltpu.VMEM((2 * n, half, wv), bf16),
            pltpu.VMEM((heads,) + square, f32),
            pltpu.VMEM((heads,) + square, f32),
            pltpu.VMEM((heads, n, BLOCK, HEAD_DIM), bf16),
        ]
        + [pltpu.VMEM((n, half, w), bf16) for w in widths]
        + [pltpu.VMEM((n, half, w), bf16) for w in widths]
        + [
            pltpu.VMEM((n, TAIL, 2 * wk + wv), bf16),
            pltpu.VMEM((CONV, 2 * wk + wv), f32),
            pltpu.VMEM((PAIR, BLOCK + 8, 2 * wk + wv), f32),
            DMA((13, n)),
            DMA((13, n)),
            DMA((13,)),
            DMA((heads,)),
            DMA((heads,)),
            DMA((heads, n)),
            DMA((heads, n)),
            DMA((heads,)),
        ],
        compiler_params=pltpu.CompilerParams(
            collective_id=0, has_side_effects=True, vmem_limit_bytes=56 * 1024 * 1024
        ),
        name="mixer",
    )(order, qkv, z, gates, conv_weight, rates, gain)


def per_device(mixed_qkv, gate_z, gate_logits, block_table, conv_weight, a_log, dt_bias, norm_gain):
    n = lax.axis_size("cp")
    segs = lax.axis_size("seg")
    heads = VALUE_HEADS // n
    blocks = 2 * n

    prior_table = lax.ppermute(block_table, "seg", [(i, (i + 1) % segs) for i in range(segs)])
    places = jnp.arange(blocks, dtype=jnp.int32)
    order = jnp.sum(
        jnp.where(block_table[0][None, :] == places[:, None], places[None, :], 0), axis=1, dtype=jnp.int32
    )
    tail_from = jnp.sum(jnp.where(prior_table[0] == blocks - 1, places, 0), dtype=jnp.int32) // 2
    order = jnp.concatenate([order, tail_from[None]])
    spare = HEAD_DIM - 2 * VALUE_HEADS
    rates = jnp.stack(
        [jnp.pad(-jnp.exp(a_log), (VALUE_HEADS, spare)), jnp.pad(dt_bias, (VALUE_HEADS, spare))]
    )
    return mixer(
        n, segs, heads, order, mixed_qkv, gate_z, gate_logits, conv_weight, rates, norm_gain[None, :]
    )


def solution(mesh):
    return jax.shard_map(
        per_device,
        mesh=mesh,
        in_specs=(
            P(("seg", "cp"), None),
            P(("seg", "cp"), None),
            P(("seg", "cp"), None),
            P("seg", None),
            P(),
            P(),
            P(),
            P(),
        ),
        out_specs=P(("seg", "cp"), None),
        check_vma=False,
    )
```

profile of v0, /device:TPU:17, one launch (start us, length us, event | category | flops | bytes accessed | tf_op | source)
XLA Modules:
  0.0 82.8 jit_solution(14763027688582415390)
XLA Ops:
  0.0 1.3 %collective-permute-start = (s32[1,16]{1,0:T(1,128)}, s32[1,16]{1,0:T(1,128)S(1)}, u32[]{:S(2)}, u32[]{:S(2)}) collective-permute-start(s32[1,16]{1,0:T(1,128)} %param.11), channel_id=1, source_target_pairs={{0,8},{8,16},{16,24},{24,0},{1,9},{9,17},{17,25},{25,1},{2,10},{10... | collective-permute-start | bytes 200 | tf_op jit(solution)/shard_map/ppermute | solution.py:502
  1.3 0.7 exponential_negate_fusion
  2.0 0.8 select_reduce_fusion
  2.7 0.7 pad_bitcast_fusion
  3.5 0.6 pad_maximum_fusion.rate_ref
  4.1 1.4 %copy.10.gates = bf16[128,64]{1,0:T(8,128)(2,1)} copy(bf16[128,64]{0,1:T(8,128)(2,1)} %param.10) | data formatting | bytes 32768 | tf_op args[2]
  5.5 0.0 collective-permute-done
  5.5 0.7 fusion
  9.0 0.6 pad_add_fusion.order
  9.6 70.9 %mixer.1 = bf16[128,4096]{1,0:T(8,128)(2,1)} custom-call(s32[17]{0:T(128)} %pad_add_fusion.order, bf16[128,8192]{1,0:T(8,128)(2,1)} %qkv.1, bf16[128,4096]{1,0:T(8,128)(2,1)} %z.1, bf16[128,64]{1,0:T(8,128)(2,1)} %copy.10.gates, f32[4,8192]{1,0:T(4,128)} %conv_weight.1, f32[2,128]{1,0:T(2,128)} %pad_maximum_fusion.rate_ref, f32[1,128]{1,0:T(1,128)} %bitcast.11), custom_call_target="tpu_custom_call" | custom-call | tf_op jit(solution)/shard_map/mixer/pallas_call | solution.py:459
  80.5 2.3 %copy.12 = bf16[128,4096]{1,0:T(8,128)(2,1)} copy(bf16[128,4096]{1,0:T(8,128)(2,1)} %mixer.1) | data formatting | bytes 2097152
Async XLA Ops:
  0.0 5.5 %collective-permute-start = (s32[1,16]{1,0:T(1,128)}, s32[1,16]{1,0:T(1,128)S(1)}, u32[]{:S(2)}, u32[]{:S(2)}) collective-permute-start(s32[1,16]{1,0:T(1,128)} %param.11), channel_id=1, source_target_pairs={{0,8},{8,16},{16,24},{24,0},{1,9},{9,17},{17,25},{25,1},{2,10},{10... | collective-permute-start | bytes 200 | tf_op jit(solution)/shard_map/ppermute | solution.py:502
where the time goes:
time: 83.1 us; the launch traced here: 82.8 us
  Pallas kernels  70.9 us (85%)
  local copies, waits for them, and re-layouts  4.45 us (5%)
  other arithmetic  3.33 us (4%)
  between operations  2.79 us (3%)
  starting transfers between devices  1.3 us (2%)
    pallas_call x1, Pallas kernels, mixer(): pl.pallas_call(functools.partial(whole_kernel, n, segs, heads), out_shape...  70.9 us
    unnamed x2, local copies, waits for them, and re-layouts  3.72 us
  transfers between devices with their start and end apart: 1, of which 0 were waited for; matrix products, arithmetic and copies ran while one was open for 5% of the time, Pallas kernels for 0%

commit v1 on v0

v1 whole, which is shorter than its diff:
```python
import functools

import jax
import jax.numpy as jnp
from jax import lax
from jax.experimental import pallas as pl
from jax.experimental.pallas import tpu as pltpu
from jax.sharding import PartitionSpec as P

VALUE_HEADS = 32
KEY_HEADS = 16
HEAD_DIM = 128
CONV = 4
BLOCK = 128
TAIL = 8
GROUP = VALUE_HEADS // KEY_HEADS
BATCH = 4

f32 = jnp.float32
bf16 = jnp.bfloat16
MESH = pl.DeviceIdType.MESH

NN = (((1,), (0,)), ((), ()))
NT = (((1,), (1,)), ((), ()))


def split(x):
    hi = x.astype(bf16)
    return hi, (x - hi.astype(f32)).astype(bf16)


def mm(a, b, dims=NN):
    def dot(x, y):
        return lax.dot_general(x, y, dims, preferred_element_type=f32)

    if dims == NT:
        return dot(a[0], b[0]) + (dot(a[0], b[1]) + dot(a[1], b[0]))
    wide = jnp.concatenate(a, axis=1)
    if b[0].shape[1] > HEAD_DIM:
        return dot(wide, jnp.concatenate([b[0], b[0]], axis=0)) + dot(a[0], b[1])
    top = jnp.concatenate([b[0], b[1]], axis=1)
    low = jnp.concatenate([b[0], jnp.zeros_like(b[1])], axis=1)
    both = dot(wide, jnp.concatenate([top, low], axis=0))
    return both[:, :HEAD_DIM] + both[:, HEAD_DIM:]


def log1p_exact(y):
    u = 1.0 + y
    return jnp.where(u == 1.0, y, jnp.log(u) * (y / jnp.where(u == 1.0, 1.0, u - 1.0)))


def scope(name):
    return jax.named_scope(name)


def squares():
    row = lax.broadcasted_iota(jnp.int32, (BLOCK, BLOCK), 0)
    col = lax.broadcasted_iota(jnp.int32, (BLOCK, BLOCK), 1)
    return row, col


def gate_terms(hpg, half_index, g, row_shift, places, gbuf, rate_ref):
    lane = lax.broadcasted_iota(jnp.int32, (8, BLOCK), 1)
    betas, decays = [], []
    for i0, i1 in places:
        found = []
        for kind in range(2):
            one = pltpu.roll(gbuf[i0, kind].astype(f32), (BLOCK // 2) * half_index, 1)
            two = pltpu.roll(gbuf[i1, kind].astype(f32), (BLOCK // 2) * (1 - half_index), 1)
            found.append(pltpu.roll(jnp.where(lane < BLOCK // 2, one, two), row_shift, 0))
        betas.append(1.0 / (1.0 + jnp.exp(-found[0])))
        shifted = found[1] + rate_ref[g, 1]
        soft = jnp.maximum(shifted, 0.0) + log1p_exact(jnp.exp(-jnp.abs(shifted)))
        decays.append(rate_ref[g, 0] * soft)
    beta = jnp.concatenate(betas, axis=0)
    decay = jnp.concatenate(decays, axis=0)
    row, col = squares()
    upto = jnp.where(row <= col, 1.0, 0.0).astype(bf16)
    d0 = decay.astype(bf16)
    rest = decay - d0.astype(f32)
    d1 = rest.astype(bf16)
    d2 = (rest - d1.astype(f32)).astype(bf16)
    cum = jnp.dot(d2, upto, preferred_element_type=f32)
    cum = cum + jnp.dot(d1, upto, preferred_element_type=f32)
    cum = cum + jnp.dot(d0, upto, preferred_element_type=f32)
    count = beta.shape[0]
    spare = jnp.zeros((BLOCK - 2 * count, BLOCK), f32)
    turned = jnp.transpose(jnp.concatenate([beta, cum, spare], axis=0))
    return cum, turned, count


def prepare(hpg, blk, g, cum, turned, count, w_ref, x_ref):
    row, col = squares()
    strict = row > col
    inclusive = row >= col

    def conv(start):
        cols = slice(start, start + HEAD_DIM)
        total_rows = w_ref[g, 0:1, cols] * x_ref[5 : 5 + BLOCK, cols]
        for j in range(1, CONV):
            total_rows = total_rows + w_ref[g, j : j + 1, cols] * x_ref[5 + j : 5 + j + BLOCK, cols]
        return total_rows / (1.0 + jnp.exp(-total_rows))

    def unit(x):
        return x * lax.rsqrt(jnp.sum(x * x, axis=-1, keepdims=True) + 1e-06)

    queries = unit(conv(0)) * HEAD_DIM ** (-0.5)
    key_rows = unit(conv(HEAD_DIM))
    ks = split(key_rows)
    qs = split(queries)
    kk = mm(ks, ks, NT)
    qk = mm(qs, ks, NT)
    lower, scores, rhs, kdt, qd, last = [], [], [], [], [], []
    for e in range(hpg):
        at = blk * 8 + e
        beta = turned[:, at : at + 1]
        c = turned[:, count + at : count + at + 1]
        ct = cum[at : at + 1, :]
        final = ct[:, BLOCK - 1 :]
        spread = c - ct
        incl = jnp.where(inclusive, jnp.exp(jnp.where(inclusive, spread, 0.0)), 0.0)
        lower.append(jnp.where(strict, beta * kk * incl, 0.0))
        scores.append(split(qk * incl))
        grow = jnp.exp(c)
        values = conv((2 + e) * HEAD_DIM)
        rhs.append(split(jnp.concatenate([values * beta, key_rows * (beta * grow)], axis=1)))
        kdt.append(split(jnp.transpose(key_rows * jnp.exp(final - c))))
        qd.append(queries * grow)
        last.append(jnp.exp(final))
    return lower, scores, rhs, kdt, qd, last


def blocks(n, hpg, g, half_index, first, row_shift, order, cur, prior, gbuf, rate_ref, w_ref, x_ref, o_ref, mh_ref, ml_ref, st_ref):
    half = cur.shape[1]
    row, col = squares()
    eye = jnp.where(row == col, 1.0, 0.0).astype(f32)
    places = [(order[2 * (first + k)], order[2 * (first + k) + 1]) for k in range(BATCH)]
    cum, turned, count = gate_terms(hpg, half_index, g, row_shift, places, gbuf, rate_ref)
    lower, scores, rhs, kdt, qd, last = [], [], [], [], [], []
    for k in range(BATCH):
        b = first + k
        if k:
            x_ref[k, 0:8, :] = cur[places[k - 1][1], half - 16 :, :].astype(f32)[8:]
        else:
            ahead = order[jnp.maximum(2 * b - 1, 0)]
            near = cur[ahead, half - 16 :, :].astype(f32)[8:]
            x_ref[k, 0:8, :] = jnp.where(lax.rem(b, n // 2) == 0, prior[...], near)
        x_ref[k, 8 : 8 + half, :] = cur[places[k][0]].astype(f32)
        x_ref[k, 8 + half : 8 + 2 * half, :] = cur[places[k][1]].astype(f32)
        found = prepare(hpg, k, g, cum, turned, count, w_ref, x_ref.at[k])
        for total, more in zip((lower, scores, rhs, kdt, qd, last), found):
            total += more
    hs = range(BATCH * hpg)

    def same(size):
        return (row // size) == (col // size)

    small = 16
    power = [split(jnp.where(same(small), -lower[h], 0.0)) for h in hs]
    inverse = [eye + jnp.where(same(small), -lower[h], 0.0) for h in hs]
    steps = 1
    while 2**steps < small:
        power = [split(mm(power[h], power[h])) for h in hs]
        inverse = [inverse[h] + mm(split(inverse[h]), power[h]) for h in hs]
        steps += 1
    size = small
    while size < BLOCK:
        between = same(2 * size) & (~same(size))
        cross = [split(jnp.where(between, lower[h], 0.0)) for h in hs]
        parts = [split(inverse[h]) for h in hs]
        mixed = [split(mm(cross[h], parts[h])) for h in hs]
        inverse = [inverse[h] - mm(parts[h], mixed[h]) for h in hs]
        size *= 2
    solved = [split(mm(split(inverse[h]), rhs[h])) for h in hs]
    outs = [mm(scores[h], solved[h]) for h in hs]
    ends = [mm(kdt[h], solved[h]) for h in hs]
    readers = [split(qd[h] - outs[h][:, HEAD_DIM:]) for h in hs]
    maps = [split(last[h] * eye - ends[h][:, HEAD_DIM:]) for h in hs]
    for k in range(BATCH):
        b = first + k
        states = [split(st_ref[g, e]) for e in range(hpg)]
        for e in range(hpg):
            at = k * hpg + e
            moved = mm(maps[at], states[e])
            st_ref[g, e] = jnp.concatenate(
                [moved[:, :HEAD_DIM] + ends[at][:, :HEAD_DIM], moved[:, HEAD_DIM:]], axis=1
            )
        for e in range(hpg):
            at = k * hpg + e
            seen = mm(readers[at], states[e])
            o_ref[g * hpg + e, b] = seen[:, :HEAD_DIM] + outs[at][:, :HEAD_DIM]
            reach = split(seen[:, HEAD_DIM:])
            mh_ref[g * hpg + e, b] = reach[0]
            ml_ref[g * hpg + e, b] = reach[1]


def whole_kernel(
    n, segs, heads, table, a_log, dt_bias, table_any, qkv, z, gates, conv_weight, gain_ref, out,
    xin, otail, gbuf, ptab, cur, prior, x_ref, w_ref, rate_ref, order, o_ref, mh_ref, ml_ref, st_ref,
    inc_ref, pass_ref, y_ref, local, lout, ssem, rsem, hsend, hrecv, *oz
):
    me = lax.axis_index("cp")
    seg = lax.axis_index("seg")
    final = segs - 1
    after = lax.rem(seg + 1, segs)
    before = lax.rem(seg + segs - 1, segs)
    keys = max(1, heads // GROUP)
    hpg = heads // keys
    units = 2 * keys
    key_width = KEY_HEADS * HEAD_DIM
    width = heads * HEAD_DIM
    wz = hpg * HEAD_DIM
    rows = qkv.shape[0]
    half = rows // 2
    AT_TAIL, AT_GATE, AT_Z, AT_TABLE, AT_Y = units, units + keys, units + keys + 1, units + 2 * keys + 1, units + 2 * keys + 2

    barrier = pltpu.get_barrier_semaphore()
    for d in range(1, n):
        pl.semaphore_signal(barrier, inc=1, device_id=(seg, lax.rem(me + d, n)), device_id_type=MESH)

    @pl.when(seg > 0)
    def _():
        for d in range(n):
            pl.semaphore_signal(barrier, inc=1, device_id=(before, lax.rem(me + d, n)), device_id_type=MESH)

    def columns(start, size):
        return pl.ds(pl.multiple_of(start, HEAD_DIM), size)

    def places(p, g):
        key = (lax.div(p * heads, GROUP) + g) * HEAD_DIM
        value = (p * heads + g * hpg) * HEAD_DIM
        return (
            (columns(key, HEAD_DIM), pl.ds(0, HEAD_DIM)),
            (columns(key_width + key, HEAD_DIM), pl.ds(HEAD_DIM, HEAD_DIM)),
            (columns(2 * key_width + value, wz), pl.ds(2 * HEAD_DIM, wz)),
        )

    def unit_pieces(p, u, slot):
        these = pl.ds((u % 2) * half, half)
        return [(qkv.at[these, src], xin.at[u, slot, :, dst]) for src, dst in places(p, u // 2)]

    def tail_pieces(p, g, slot):
        these = pl.ds(rows - TAIL, TAIL)
        return [(qkv.at[these, src], otail.at[g, slot, :, dst]) for src, dst in places(p, g)]

    def gate_pieces(p, slot):
        tile = lax.div(p * heads, 8) * 8
        return [
            (gates.at[pl.ds(pl.multiple_of(kind * VALUE_HEADS + tile, 8), 8)], gbuf.at[slot, kind]) for kind in range(2)
        ]

    def z_pieces(p, g, slot):
        cols = columns((p * heads + g * hpg) * HEAD_DIM, wz)
        return [(z.at[pl.ds(hf * half, half), cols], oz[g].at[slot, hf]) for hf in range(2)]

    for g in range(keys):
        for src, dst in places(me, g):
            pltpu.make_async_copy(conv_weight.at[:, src], w_ref.at[g, :, dst], lout.at[0]).start()
    for kind, found in enumerate(
        [unit_pieces(me, u, me) for u in range(units)]
        + [gate_pieces(me, me)]
        + [z_pieces(me, g, me) for g in range(keys)]
    ):
        for src, dst in found:
            pltpu.make_async_copy(src, dst, local.at[kind]).start()
    with scope("entry"):
        pl.semaphore_wait(barrier, n - 1 + jnp.where(seg < final, n, 0))

    def post(kind, src, dst, target):
        pltpu.make_async_remote_copy(
            src_ref=src, dst_ref=dst, send_sem=ssem.at[kind], recv_sem=rsem.at[kind],
            device_id=target, device_id_type=MESH,
        ).start()

    def remote(kind, ref):
        return pltpu.make_async_remote_copy(
            src_ref=ref, dst_ref=ref, send_sem=ssem.at[kind], recv_sem=rsem.at[kind],
            device_id=(seg, lax.rem(me + 1, n)), device_id_type=MESH,
        )

    others = pl.ds(0, n - 1)

    def post_tails(g):
        @pl.when(seg < final)
        def _():
            if g == 0:
                post(AT_TABLE, table_any, ptab, (after, me))
            for d in range(n):
                peer = lax.rem(me + d, n)
                for src, dst in tail_pieces(peer, g, me):
                    post(AT_TAIL + g, src, dst, (after, peer))

    def post_all(kind, find):
        for d in range(1, n):
            peer = lax.rem(me + d, n)
            for src, dst in find(peer):
                post(kind, src, dst, (seg, peer))

    post_all(AT_GATE, lambda p: gate_pieces(p, me))
    for g in range(keys):
        post_tails(g)
        for u in (2 * g, 2 * g + 1):
            post_all(u, lambda p: unit_pieces(p, u, me))
    for g in range(keys):
        post_all(AT_Z + g, lambda p: z_pieces(p, g, me))

    def find(b, carry):
        parity = lax.div(b, n)
        place = jnp.int32(0)
        for j in range(n):
            place = jnp.where(table[0, 2 * j + parity] == b, j, place)
        order[b] = place
        return carry

    lax.fori_loop(0, 2 * n, find, 0)

    row, col = squares()
    line = lax.broadcasted_iota(jnp.int32, (8, BLOCK), 0)
    for g in range(keys):
        scale = jnp.zeros((8, BLOCK), f32)
        shift = jnp.zeros((8, BLOCK), f32)
        for e in range(hpg):
            h = me * heads + g * hpg + e
            scale = jnp.where(line == e, a_log[h], scale)
            shift = jnp.where(line == e, dt_bias[h], shift)
            st_ref[g, e, :, :HEAD_DIM] = jnp.zeros((HEAD_DIM, HEAD_DIM), f32)
            st_ref[g, e, :, HEAD_DIM:] = jnp.where(row == col, 1.0, 0.0).astype(f32)
        rate_ref[g, 0] = -jnp.exp(scale)
        rate_ref[g, 1] = shift

    pltpu.make_async_copy(w_ref, w_ref, lout.at[0]).wait()
    pltpu.make_async_copy(gbuf.at[me], gbuf.at[me], local.at[units]).wait()
    with scope("gatewait"):
        remote(AT_GATE, gbuf.at[others]).wait_recv()

    @pl.when(seg > 0)
    def _():
        remote(AT_TABLE, ptab).wait_recv()

    def hop(h):
        return pltpu.make_async_remote_copy(
            src_ref=pass_ref.at[h],
            dst_ref=inc_ref.at[h],
            send_sem=hsend.at[h],
            recv_sem=hrecv.at[h],
            device_id=(after, me),
            device_id_type=MESH,
        )

    def forward(g):
        @pl.when(seg == 0)
        def _():
            for e in range(hpg):
                h = g * hpg + e
                pass_ref[h] = st_ref[g, e, :, :HEAD_DIM]
                hop(h).start()

        @pl.when((seg > 0) & (seg < final))
        def _():
            for e in range(hpg):
                h = g * hpg + e
                through = split(st_ref[g, e, :, HEAD_DIM:])
                with scope("hopmid"):
                    hop(h).wait_recv()
                pass_ref[h] = st_ref[g, e, :, :HEAD_DIM] + mm(through, split(inc_ref[h]))
                hop(h).start()

    def one_unit(u, carry):
        g = lax.div(u, 2)
        half_index = lax.rem(u, 2)
        with scope("unitwait"):
            pltpu.make_async_copy(xin.at[u, me], xin.at[u, me], local.at[u]).wait()
            remote(u, xin.at[u, others]).wait_recv()

        @pl.when((half_index == 0) & (seg == 0))
        def _():
            prior[...] = jnp.zeros_like(prior)

        @pl.when((half_index == 0) & (seg > 0))
        def _():
            with scope("tailwait"):
                remote(AT_TAIL + g, otail.at[g]).wait_recv()
            found = jnp.zeros(prior.shape, f32)
            for j in range(n):
                hit = ptab[0:1, 2 * j + 1 : 2 * j + 2] == 2 * n - 1
                found = jnp.where(hit, otail[g, j].astype(f32), found)
            prior[...] = found

        @pl.when(half_index == 1)
        def _():
            prior[...] = cur[order[n - 1], half - 16 :, :].astype(f32)[8:]

        cur[...] = xin[u]
        row_shift = lax.rem(8 - lax.rem(me * heads, 8) - g * hpg + 8, 8)

        def batch(first):
            blocks(
                n, hpg, g, half_index, first, row_shift, order, cur, prior, gbuf, rate_ref,
                w_ref, x_ref, o_ref, mh_ref, ml_ref, st_ref,
            )

        turns = n // 2 // BATCH
        with scope("run"):
            if turns == 1:
                batch(half_index * (n // 2))
            else:
                lax.fori_loop(0, turns, lambda t, c: (batch(half_index * (n // 2) + t * BATCH), c)[1], 0)
        for earlier in range(keys - 1):
            @pl.when(u == jnp.minimum(2 * earlier + 1 + seg, units - 1))
            def _():
                forward(earlier)
        return carry

    lax.fori_loop(0, units, one_unit, 0)

    def block(h, b, state):
        g, e = h // hpg, h % hpg
        i0 = order[2 * b]
        i1 = order[2 * b + 1]
        which = lax.div(b, n // 2)
        cols = pl.ds(e * HEAD_DIM, HEAD_DIM)
        core = o_ref[h, b] + mm((mh_ref[h, b], ml_ref[h, b]), state)
        gate = jnp.concatenate([oz[g][i0, which, :, cols], oz[g][i1, which, :, cols]], axis=0).astype(f32)
        scale = lax.rsqrt(jnp.sum(core * core, axis=-1, keepdims=True) * (1.0 / HEAD_DIM) + 1e-06)
        y_ref[h, b] = (core * scale * gain_ref[0:1, :] * (gate / (1.0 + jnp.exp(-gate)))).astype(bf16)

    def target(h, source):
        return out.at[:, columns(source * width + h * HEAD_DIM, HEAD_DIM)]

    def give(h, d):
        peer = lax.rem(me + d, n)
        post(AT_Y, y_ref.at[h, peer], target(h, me), (seg, peer))

    def close(h):
        @pl.when(seg == 0)
        def _():
            inc_ref[h] = jnp.zeros((HEAD_DIM, HEAD_DIM), f32)

        @pl.when(seg == final)
        def _():
            with scope("hoplast"):
                hop(h).wait_recv()

        state = split(inc_ref[h])
        for d in range(1, n):
            block(h, lax.rem(me + d, n), state)
            if d > 1:
                give(h, d - 1)
        block(h, me, state)
        give(h, n - 1)
        pltpu.make_async_copy(y_ref.at[h, me], target(h, me), lout.at[1]).start()

    for h in range(heads):
        g = h // hpg
        if h % hpg == 0:
            for kind in (AT_Z + g,):
                pltpu.make_async_copy(oz[g].at[me], oz[g].at[me], local.at[units + 1 + g]).wait()
                with scope("zwait"):
                    remote(kind, oz[g].at[others]).wait_recv()
        if h == min(hpg, heads - hpg):
            with scope("forward_late"):
                pl.when(seg > 1)(lambda: forward(keys - 1))
        if h == 0:
            with scope("forward_early"):
                pl.when(seg <= 1)(lambda: forward(keys - 1))
        with scope("close"):
            close(h)

    with scope("waity"):
        pltpu.make_async_copy(y_ref.at[:, 0], y_ref.at[:, 0], lout.at[1]).wait()
        remote(AT_Y, y_ref.at[:, others]).wait_recv()
    with scope("drain"):
        remote(AT_GATE, gbuf.at[others]).wait_send()
        for u in range(units):
            remote(u, xin.at[u, others]).wait_send()
        for g in range(keys):
            remote(AT_Z + g, oz[g].at[others]).wait_send()
        remote(AT_Y, y_ref.at[:, others]).wait_send()

        @pl.when(seg < final)
        def _():
            remote(AT_TABLE, ptab).wait_send()
            for g in range(keys):
                remote(AT_TAIL + g, otail.at[g]).wait_send()
            for h in range(heads):
                hop(h).wait_send()


def mixer(n, segs, heads, table, a_log, dt_bias, qkv, z, gates, conv_weight, gain):
    keys = max(1, heads // GROUP)
    hpg = heads // keys
    units = 2 * keys
    half = qkv.shape[0] // 2
    wide = (2 + hpg) * HEAD_DIM
    anywhere = pl.BlockSpec(memory_space=pl.ANY)
    vmem = pl.BlockSpec(memory_space=pltpu.VMEM)
    smem = pl.BlockSpec(memory_space=pltpu.SMEM)
    square = (HEAD_DIM, HEAD_DIM)
    DMA = pltpu.SemaphoreType.DMA
    kinds = units + 2 * keys + 3
    return pl.pallas_call(
        functools.partial(whole_kernel, n, segs, heads),
        out_shape=pltpu.VMEM((BLOCK, n * heads * HEAD_DIM), bf16),
        in_specs=[smem] * 3 + [anywhere] * 5 + [vmem],
        out_specs=vmem,
        scratch_shapes=[
            pltpu.VMEM((units, n, half, wide), bf16),
            pltpu.VMEM((keys, n, TAIL, wide), bf16),
            pltpu.VMEM((n, 2, 8, BLOCK), bf16),
            pltpu.VMEM(table.shape, jnp.int32),
            pltpu.VMEM((n, half, wide), bf16),
            pltpu.VMEM((TAIL, wide), f32),
            pltpu.VMEM((BATCH, BLOCK + 8, wide), f32),
            pltpu.VMEM((keys, CONV, wide), f32),
            pltpu.VMEM((keys, 2, 8, BLOCK), f32),
            pltpu.SMEM((2 * n,), jnp.int32),
            pltpu.VMEM((heads, n) + square, f32),
            pltpu.VMEM((heads, n) + square, bf16),
            pltpu.VMEM((heads, n) + square, bf16),
            pltpu.VMEM((keys, hpg, HEAD_DIM, 2 * HEAD_DIM), f32),
            pltpu.VMEM((heads,) + square, f32),
            pltpu.VMEM((heads,) + square, f32),
            pltpu.VMEM((heads, n) + square, bf16),
            DMA((units + 1 + keys,)),
            DMA((2,)),
            DMA((kinds,)),
            DMA((kinds,)),
            DMA((heads,)),
            DMA((heads,)),
        ]
        + [pltpu.VMEM((n, 2, half, hpg * HEAD_DIM), bf16)] * keys,
        compiler_params=pltpu.CompilerParams(
            collective_id=0, has_side_effects=True, vmem_limit_bytes=48 * 1024 * 1024
        ),
        name="mixer",
    )(*[pltpu.with_memory_space_constraint(x, pltpu.HBM) for x in (table, a_log, dt_bias, table, qkv, z, gates, conv_weight, gain)])


def per_device(mixed_qkv, gate_z, gate_logits, block_table, conv_weight, a_log, dt_bias, norm_gain):
    n = lax.axis_size("cp")
    segs = lax.axis_size("seg")
    return mixer(
        n, segs, VALUE_HEADS // n, block_table, a_log, dt_bias, mixed_qkv, gate_z, gate_logits.T,
        conv_weight, norm_gain[None, :],
    )


def solution(mesh):
    return jax.shard_map(
        per_device,
        mesh=mesh,
        in_specs=(
            P(("seg", "cp"), None),
            P(("seg", "cp"), None),
            P(("seg", "cp"), None),
            P("seg", None),
            P(),
            P(),
            P(),
            P(),
        ),
        out_specs=P(("seg", "cp"), None),
        check_vma=False,
    )
```

time: 83.1 us -> 54.7 us (0.66)
  Pallas kernels: 70.9 us -> 53.2 us
  local copies, waits for them, and re-layouts: 4.45 us -> 0.97 us
  other arithmetic: 3.33 us -> 0 us
  between operations: 2.79 us -> 0.01 us
  starting transfers between devices: 1.3 us -> 0 us
    pallas_call x1, Pallas kernels: 70.9 us -> 53.2 us  [mixer(): pl.pallas_call(functools.partial(whole_kernel, n, segs, heads), out_shape...]
    unnamed x2 -> x1, local copies, waits for them, and re-layouts: 3.72 us -> 0.97 us
    reduce_sum x2 -> x0, other arithmetic: 1.49 us -> none  [the longest x1 0.77 us: per_device(): jnp.sum(jnp.where(block_table[0][None, :] == places[:, None], places[None...]
    ppermute x1 -> x0, starting transfers between devices: 1.3 us -> none  [per_device(): lax.ppermute(block_table, 'seg', [(i, (i + 1) % segs) for i in range(segs)])]
  transfers between devices with their start and end apart: 1 -> 0, of which waited for: 0 -> 0; matrix products, arithmetic and copies ran while one was open for 5% -> 0% of each run, Pallas kernels for 0% -> 0%
where the time goes in v1:
time: 54.7 us; the launch traced here: 54.2 us
  Pallas kernels  53.2 us (97%)
  local copies, waits for them, and re-layouts  0.97 us (2%)
    pallas_call x1, Pallas kernels, mixer(): pl.pallas_call(functools.partial(whole_kernel, n, segs, heads), out_shape...  53.2 us

profile of v1, /device:TPU:17, one launch (start us, length us, event | category | flops | bytes accessed | tf_op | source)
XLA Modules:
  0.0 54.2 jit_solution(11079735390660510160)
XLA Ops:
  0.0 53.2 %mixer.1 = bf16[128,4096]{1,0:T(8,128)(2,1)S(1)} custom-call(s32[1,16]{1,0:T(1,128)} %table_any.1, f32[32]{0:T(128)} %a_log.1, f32[32]{0:T(128)} %dt_bias.1, s32[1,16]{1,0:T(1,128)} %table_any.1, bf16[128,8192]{1,0:T(8,128)(2,1)} %qkv.1, bf16[128,4096]{1,0:T(8,128)(2,1)} %z.1, bf16[64,128]{1,0:T(8,128)(2,1)} %bitcast.2, f32[4,8192]{1,0:T(4,128)} %conv_weight.1, ...), custom_call_target="tpu_custom_call" | custom-call | tf_op jit(solution)/shard_map/mixer/pallas_call | solution.py:501
  53.3 1.0 %copy.10 = bf16[128,4096]{1,0:T(8,128)(2,1)} copy(bf16[128,4096]{1,0:T(8,128)(2,1)S(1)} %mixer.1) | data formatting | bytes 2097152

commit v2 on v1

--- a/solution.py
+++ b/solution.py
@@ -195,9 +195,10 @@
 
 
 def whole_kernel(
-    n, segs, heads, table, a_log, dt_bias, table_any, qkv, z, gates, conv_weight, gain_ref, out,
+    n, segs, heads, table_any, a_log_any, dt_bias_any, qkv, z, gates, conv_weight, gain_any, out,
+    table, a_log, dt_bias, gain_ref, stage, gstage, tstage, tsend,
     xin, otail, gbuf, ptab, cur, prior, x_ref, w_ref, rate_ref, order, o_ref, mh_ref, ml_ref, st_ref,
-    inc_ref, pass_ref, y_ref, local, lout, ssem, rsem, hsend, hrecv, *oz
+    inc_ref, pass_ref, y_ref, lin, local, lout, ssem, rsem, hsend, hrecv, ready, *oz
 ):
     me = lax.axis_index("cp")
     seg = lax.axis_index("seg")
@@ -218,10 +219,26 @@
     for d in range(1, n):
         pl.semaphore_signal(barrier, inc=1, device_id=(seg, lax.rem(me + d, n)), device_id_type=MESH)
 
-    @pl.when(seg > 0)
+    @pl.when(seg < final)
     def _():
-        for d in range(n):
-            pl.semaphore_signal(barrier, inc=1, device_id=(before, lax.rem(me + d, n)), device_id_type=MESH)
+        pl.semaphore_signal(barrier, inc=1, device_id=(after, me), device_id_type=MESH)
+
+    small = [
+        pltpu.make_async_copy(src, dst, lin.at[i])
+        for i, (src, dst) in enumerate(
+            (
+                (qkv.at[pl.ds(0, half)], stage),
+                (gates, gstage),
+                (qkv.at[pl.ds(rows - TAIL, TAIL)], tstage),
+                (table_any, table),
+                (a_log_any, a_log),
+                (dt_bias_any, dt_bias),
+                (gain_any, gain_ref),
+            )
+        )
+    ]
+    for copy in small:
+        copy.start()
 
     def columns(start, size):
         return pl.ds(pl.multiple_of(start, HEAD_DIM), size)
@@ -236,17 +253,14 @@
         )
 
     def unit_pieces(p, u, slot):
-        these = pl.ds((u % 2) * half, half)
-        return [(qkv.at[these, src], xin.at[u, slot, :, dst]) for src, dst in places(p, u // 2)]
-
-    def tail_pieces(p, g, slot):
-        these = pl.ds(rows - TAIL, TAIL)
-        return [(qkv.at[these, src], otail.at[g, slot, :, dst]) for src, dst in places(p, g)]
+        if u % 2 == 0:
+            return [(stage.at[:, src], xin.at[u, slot, :, dst]) for src, dst in places(p, u // 2)]
+        return [(qkv.at[pl.ds(half, half), src], xin.at[u, slot, :, dst]) for src, dst in places(p, u // 2)]
 
     def gate_pieces(p, slot):
         tile = lax.div(p * heads, 8) * 8
         return [
-            (gates.at[pl.ds(pl.multiple_of(kind * VALUE_HEADS + tile, 8), 8)], gbuf.at[slot, kind]) for kind in range(2)
+            (gstage.at[pl.ds(pl.multiple_of(kind * VALUE_HEADS + tile, 8), 8)], gbuf.at[slot, kind]) for kind in range(2)
         ]
 
     def z_pieces(p, g, slot):
@@ -256,6 +270,8 @@
     for g in range(keys):
         for src, dst in places(me, g):
             pltpu.make_async_copy(conv_weight.at[:, src], w_ref.at[g, :, dst], lout.at[0]).start()
+    small[0].wait()
+    small[1].wait()
     for kind, found in enumerate(
         [unit_pieces(me, u, me) for u in range(units)]
         + [gate_pieces(me, me)]
@@ -264,7 +280,11 @@
         for src, dst in found:
             pltpu.make_async_copy(src, dst, local.at[kind]).start()
     with scope("entry"):
-        pl.semaphore_wait(barrier, n - 1 + jnp.where(seg < final, n, 0))
+        pl.semaphore_wait(barrier, n - 1 + jnp.where(seg > 0, 1, 0))
+
+    @pl.when(seg > 0)
+    def _():
+        pl.semaphore_signal(ready, inc=1, device_id=(before, me), device_id_type=MESH)
 
     def post(kind, src, dst, target):
         pltpu.make_async_remote_copy(
@@ -280,16 +300,6 @@
 
     others = pl.ds(0, n - 1)
 
-    def post_tails(g):
-        @pl.when(seg < final)
-        def _():
-            if g == 0:
-                post(AT_TABLE, table_any, ptab, (after, me))
-            for d in range(n):
-                peer = lax.rem(me + d, n)
-                for src, dst in tail_pieces(peer, g, me):
-                    post(AT_TAIL + g, src, dst, (after, peer))
-
     def post_all(kind, find):
         for d in range(1, n):
             peer = lax.rem(me + d, n)
@@ -297,10 +307,35 @@
                 post(kind, src, dst, (seg, peer))
 
     post_all(AT_GATE, lambda p: gate_pieces(p, me))
+    post_all(0, lambda p: unit_pieces(p, 0, me))
+    for copy in small[2:]:
+        copy.wait()
+
+    wide = hpg + 2
+    pairs = (wide + 1) // 2
+    upper = lax.broadcasted_iota(jnp.int32, (TAIL, HEAD_DIM), 0) < TAIL // 2
     for g in range(keys):
-        post_tails(g)
-        for u in (2 * g, 2 * g + 1):
-            post_all(u, lambda p: unit_pieces(p, u, me))
+        for p in range(n):
+            key = p * heads // GROUP + g
+            at = [key, KEY_HEADS + key] + [2 * KEY_HEADS + p * heads + g * hpg + e for e in range(hpg)]
+            tiles = [tstage[:, i * HEAD_DIM : (i + 1) * HEAD_DIM].astype(f32) for i in at]
+            for i in range(pairs):
+                low = tiles[i + pairs] if i + pairs < wide else tiles[i]
+                both = jnp.where(upper, pltpu.roll(tiles[i], TAIL // 2, 0), low)
+                tsend[g, p, :, i * HEAD_DIM : (i + 1) * HEAD_DIM] = both.astype(bf16)
+
+    @pl.when(seg < final)
+    def _():
+        with scope("readywait"):
+            pl.semaphore_wait(ready, 1)
+        post(AT_TABLE, table_any, ptab, (after, me))
+        for g in range(keys):
+            for d in range(n):
+                peer = lax.rem(me + d, n)
+                post(AT_TAIL + g, tsend.at[g, peer], otail.at[g, me], (after, peer))
+
+    for u in range(1, units):
+        post_all(u, lambda p: unit_pieces(p, u, me))
     for g in range(keys):
         post_all(AT_Z + g, lambda p: z_pieces(p, g, me))
 
@@ -380,11 +415,13 @@
         def _():
             with scope("tailwait"):
                 remote(AT_TAIL + g, otail.at[g]).wait_recv()
-            found = jnp.zeros(prior.shape, f32)
+            found = jnp.zeros(otail.shape[2:], f32)
             for j in range(n):
                 hit = ptab[0:1, 2 * j + 1 : 2 * j + 2] == 2 * n - 1
                 found = jnp.where(hit, otail[g, j].astype(f32), found)
-            prior[...] = found
+            for i in range(wide):
+                pair = found[:, i % pairs * HEAD_DIM : (i % pairs + 1) * HEAD_DIM]
+                prior[:, i * HEAD_DIM : (i + 1) * HEAD_DIM] = pltpu.roll(pair, TAIL // 2, 0) if i < pairs else pair
 
         @pl.when(half_index == 1)
         def _():
@@ -452,17 +489,15 @@
 
     for h in range(heads):
         g = h // hpg
+        late = heads - hpg
+        for turn in range(late + 1):
+            if h == turn:
+                with scope("forward"):
+                    pl.when(jnp.minimum(seg, late) == turn)(lambda: forward(keys - 1))
         if h % hpg == 0:
-            for kind in (AT_Z + g,):
-                pltpu.make_async_copy(oz[g].at[me], oz[g].at[me], local.at[units + 1 + g]).wait()
-                with scope("zwait"):
-                    remote(kind, oz[g].at[others]).wait_recv()
-        if h == min(hpg, heads - hpg):
-            with scope("forward_late"):
-                pl.when(seg > 1)(lambda: forward(keys - 1))
-        if h == 0:
-            with scope("forward_early"):
-                pl.when(seg <= 1)(lambda: forward(keys - 1))
+            pltpu.make_async_copy(oz[g].at[me], oz[g].at[me], local.at[units + 1 + g]).wait()
+            with scope("zwait"):
+                remote(AT_Z + g, oz[g].at[others]).wait_recv()
         with scope("close"):
             close(h)
 
@@ -492,20 +527,28 @@
     units = 2 * keys
     half = qkv.shape[0] // 2
     wide = (2 + hpg) * HEAD_DIM
+    packed = (3 + hpg) // 2 * HEAD_DIM
     anywhere = pl.BlockSpec(memory_space=pl.ANY)
     vmem = pl.BlockSpec(memory_space=pltpu.VMEM)
-    smem = pl.BlockSpec(memory_space=pltpu.SMEM)
     square = (HEAD_DIM, HEAD_DIM)
     DMA = pltpu.SemaphoreType.DMA
     kinds = units + 2 * keys + 3
     return pl.pallas_call(
         functools.partial(whole_kernel, n, segs, heads),
         out_shape=pltpu.VMEM((BLOCK, n * heads * HEAD_DIM), bf16),
-        in_specs=[smem] * 3 + [anywhere] * 5 + [vmem],
+        in_specs=[anywhere] * 8,
         out_specs=vmem,
         scratch_shapes=[
+            pltpu.SMEM(table.shape, jnp.int32),
+            pltpu.SMEM(a_log.shape, f32),
+            pltpu.SMEM(dt_bias.shape, f32),
+            pltpu.VMEM(gain.shape, f32),
+            pltpu.VMEM((half, qkv.shape[1]), bf16),
+            pltpu.VMEM(gates.shape, bf16),
+            pltpu.VMEM((TAIL, qkv.shape[1]), bf16),
+            pltpu.VMEM((keys, n, TAIL, packed), bf16),
             pltpu.VMEM((units, n, half, wide), bf16),
-            pltpu.VMEM((keys, n, TAIL, wide), bf16),
+            pltpu.VMEM((keys, n, TAIL, packed), bf16),
             pltpu.VMEM((n, 2, 8, BLOCK), bf16),
             pltpu.VMEM(table.shape, jnp.int32),
             pltpu.VMEM((n, half, wide), bf16),
@@ -521,19 +564,21 @@
             pltpu.VMEM((heads,) + square, f32),
             pltpu.VMEM((heads,) + square, f32),
             pltpu.VMEM((heads, n) + square, bf16),
+            DMA((7,)),
             DMA((units + 1 + keys,)),
             DMA((2,)),
             DMA((kinds,)),
             DMA((kinds,)),
             DMA((heads,)),
             DMA((heads,)),
+            pltpu.SemaphoreType.REGULAR,
         ]
         + [pltpu.VMEM((n, 2, half, hpg * HEAD_DIM), bf16)] * keys,
         compiler_params=pltpu.CompilerParams(
             collective_id=0, has_side_effects=True, vmem_limit_bytes=48 * 1024 * 1024
         ),
         name="mixer",
-    )(*[pltpu.with_memory_space_constraint(x, pltpu.HBM) for x in (table, a_log, dt_bias, table, qkv, z, gates, conv_weight, gain)])
+    )(*[pltpu.with_memory_space_constraint(x, pltpu.HBM) for x in (table, a_log, dt_bias, qkv, z, gates, conv_weight, gain)])
 
 
 def per_device(mixed_qkv, gate_z, gate_logits, block_table, conv_weight, a_log, dt_bias, norm_gain):

time: 54.7 us -> 52.2 us (0.954)
  Pallas kernels: 53.2 us -> 50.6 us
    pallas_call x1, Pallas kernels: 53.2 us -> 50.6 us  [mixer(): pl.pallas_call(functools.partial(whole_kernel, n, segs, heads), out_shape...]
where the time goes in v2:
time: 52.2 us; the launch traced here: 51.6 us
  Pallas kernels  50.6 us (97%)
  local copies, waits for them, and re-layouts  0.97 us (2%)
    pallas_call x1, Pallas kernels, mixer(): pl.pallas_call(functools.partial(whole_kernel, n, segs, heads), out_shape...  50.6 us

profile of v2, /device:TPU:17, one launch (start us, length us, event | category | flops | bytes accessed | tf_op | source)
XLA Modules:
  0.0 51.6 jit_solution(17873054261899842853)
XLA Ops:
  0.0 50.6 %mixer.1 = bf16[128,4096]{1,0:T(8,128)(2,1)S(1)} custom-call(s32[1,16]{1,0:T(1,128)} %table_any.1, f32[32]{0:T(128)} %a_log_any.1, f32[32]{0:T(128)} %dt_bias_any.1, bf16[128,8192]{1,0:T(8,128)(2,1)} %qkv.1, bf16[128,4096]{1,0:T(8,128)(2,1)} %z.1, bf16[64,128]{1,0:T(8,128)(2,1)} %bitcast.2, f32[4,8192]{1,0:T(4,128)} %conv_weight.1, f32[1,128]{1,0:T(1,128)} %bitcast.3), custom_call_target="tpu_custom_call" | custom-call | tf_op jit(solution)/shard_map/mixer/pallas_call | solution.py:536
  50.6 1.0 %copy.10 = bf16[128,4096]{1,0:T(8,128)(2,1)} copy(bf16[128,4096]{1,0:T(8,128)(2,1)S(1)} %mixer.1) | data formatting | bytes 2097152

commit v3 on v2

--- a/solution.py
+++ b/solution.py
@@ -63,13 +63,11 @@
     lane = lax.broadcasted_iota(jnp.int32, (8, BLOCK), 1)
     betas, decays = [], []
     for i0, i1 in places:
-        found = []
-        for kind in range(2):
-            one = pltpu.roll(gbuf[i0, kind].astype(f32), (BLOCK // 2) * half_index, 1)
-            two = pltpu.roll(gbuf[i1, kind].astype(f32), (BLOCK // 2) * (1 - half_index), 1)
-            found.append(pltpu.roll(jnp.where(lane < BLOCK // 2, one, two), row_shift, 0))
-        betas.append(1.0 / (1.0 + jnp.exp(-found[0])))
-        shifted = found[1] + rate_ref[g, 1]
+        one = pltpu.roll(gbuf[i0].astype(f32), (BLOCK // 2) * half_index, 1)
+        two = pltpu.roll(gbuf[i1].astype(f32), (BLOCK // 2) * (1 - half_index), 1)
+        found = pltpu.roll(jnp.where(lane < BLOCK // 2, one, two), row_shift, 0)
+        betas.append(1.0 / (1.0 + jnp.exp(-found)))
+        shifted = pltpu.roll(found, 4, 0) + rate_ref[g, 1]
         soft = jnp.maximum(shifted, 0.0) + log1p_exact(jnp.exp(-jnp.abs(shifted)))
         decays.append(rate_ref[g, 0] * soft)
     beta = jnp.concatenate(betas, axis=0)
@@ -196,9 +194,9 @@
 
 def whole_kernel(
     n, segs, heads, table_any, a_log_any, dt_bias_any, qkv, z, gates, conv_weight, gain_any, out,
-    table, a_log, dt_bias, gain_ref, stage, gstage, tstage, tsend,
+    table, a_log, dt_bias, gain_ref, stage, gstage, gsend, tstage, tsend,
     xin, otail, gbuf, ptab, cur, prior, x_ref, w_ref, rate_ref, order, o_ref, mh_ref, ml_ref, st_ref,
-    inc_ref, pass_ref, y_ref, lin, local, lout, ssem, rsem, hsend, hrecv, ready, *oz
+    inc_ref, pass_ref, y_ref, lin, lout, ssem, rsem, hsend, hrecv, ready, *oz
 ):
     me = lax.axis_index("cp")
     seg = lax.axis_index("seg")
@@ -227,8 +225,8 @@
         pltpu.make_async_copy(src, dst, lin.at[i])
         for i, (src, dst) in enumerate(
             (
+                (gates, gstage),
                 (qkv.at[pl.ds(0, half)], stage),
-                (gates, gstage),
                 (qkv.at[pl.ds(rows - TAIL, TAIL)], tstage),
                 (table_any, table),
                 (a_log_any, a_log),
@@ -258,10 +256,7 @@
         return [(qkv.at[pl.ds(half, half), src], xin.at[u, slot, :, dst]) for src, dst in places(p, u // 2)]
 
     def gate_pieces(p, slot):
-        tile = lax.div(p * heads, 8) * 8
-        return [
-            (gstage.at[pl.ds(pl.multiple_of(kind * VALUE_HEADS + tile, 8), 8)], gbuf.at[slot, kind]) for kind in range(2)
-        ]
+        return [(gsend.at[p], gbuf.at[slot])]
 
     def z_pieces(p, g, slot):
         cols = columns((p * heads + g * hpg) * HEAD_DIM, wz)
@@ -269,16 +264,22 @@
 
     for g in range(keys):
         for src, dst in places(me, g):
-            pltpu.make_async_copy(conv_weight.at[:, src], w_ref.at[g, :, dst], lout.at[0]).start()
+            pltpu.make_async_copy(conv_weight.at[:, src], w_ref.at[g, :, dst], lout).start()
     small[0].wait()
+    line = lax.broadcasted_iota(jnp.int32, (8, BLOCK), 0)
+    for p in range(n):
+        tile = p * heads // 8 * 8
+        shift = p * heads % 8
+        strength = pltpu.roll(gstage[tile : tile + 8].astype(f32), (8 - shift) % 8, 0)
+        decay = pltpu.roll(gstage[VALUE_HEADS + tile : VALUE_HEADS + tile + 8].astype(f32), (12 - shift) % 8, 0)
+        gsend[p] = jnp.where(line < 4, strength, decay).astype(bf16)
+    gbuf[me] = gsend[me]
     small[1].wait()
-    for kind, found in enumerate(
-        [unit_pieces(me, u, me) for u in range(units)]
-        + [gate_pieces(me, me)]
-        + [z_pieces(me, g, me) for g in range(keys)]
-    ):
+    for kind, found in [(u, unit_pieces(me, u, me)) for u in range(units)] + [
+        (AT_Z + g, z_pieces(me, g, me)) for g in range(keys)
+    ]:
         for src, dst in found:
-            pltpu.make_async_copy(src, dst, local.at[kind]).start()
+            pltpu.make_async_copy(src, dst, rsem.at[kind]).start()
     with scope("entry"):
         pl.semaphore_wait(barrier, n - 1 + jnp.where(seg > 0, 1, 0))
 
@@ -286,15 +287,20 @@
     def _():
         pl.semaphore_signal(ready, inc=1, device_id=(before, me), device_id_type=MESH)
 
+    def shared(kind):
+        if not isinstance(kind, int):
+            return 0
+        return 0 if kind < units else 1 if kind < units + keys else kind - units - keys + 2
+
     def post(kind, src, dst, target):
         pltpu.make_async_remote_copy(
-            src_ref=src, dst_ref=dst, send_sem=ssem.at[kind], recv_sem=rsem.at[kind],
+            src_ref=src, dst_ref=dst, send_sem=ssem.at[shared(kind)], recv_sem=rsem.at[kind],
             device_id=target, device_id_type=MESH,
         ).start()
 
     def remote(kind, ref):
         return pltpu.make_async_remote_copy(
-            src_ref=ref, dst_ref=ref, send_sem=ssem.at[kind], recv_sem=rsem.at[kind],
+            src_ref=ref, dst_ref=ref, send_sem=ssem.at[shared(kind)], recv_sem=rsem.at[kind],
             device_id=(seg, lax.rem(me + 1, n)), device_id_type=MESH,
         )
 
@@ -350,7 +356,6 @@
     lax.fori_loop(0, 2 * n, find, 0)
 
     row, col = squares()
-    line = lax.broadcasted_iota(jnp.int32, (8, BLOCK), 0)
     for g in range(keys):
         scale = jnp.zeros((8, BLOCK), f32)
         shift = jnp.zeros((8, BLOCK), f32)
@@ -363,8 +368,7 @@
         rate_ref[g, 0] = -jnp.exp(scale)
         rate_ref[g, 1] = shift
 
-    pltpu.make_async_copy(w_ref, w_ref, lout.at[0]).wait()
-    pltpu.make_async_copy(gbuf.at[me], gbuf.at[me], local.at[units]).wait()
+    pltpu.make_async_copy(w_ref, w_ref, lout).wait()
     with scope("gatewait"):
         remote(AT_GATE, gbuf.at[others]).wait_recv()
 
@@ -376,14 +380,14 @@
         return pltpu.make_async_remote_copy(
             src_ref=pass_ref.at[h],
             dst_ref=inc_ref.at[h],
-            send_sem=hsend.at[h],
+            send_sem=hsend,
             recv_sem=hrecv.at[h],
             device_id=(after, me),
             device_id_type=MESH,
         )
 
     def forward(g):
-        @pl.when(seg == 0)
+        @pl.when((seg == 0) & (seg < final))
         def _():
             for e in range(hpg):
                 h = g * hpg + e
@@ -404,8 +408,7 @@
         g = lax.div(u, 2)
         half_index = lax.rem(u, 2)
         with scope("unitwait"):
-            pltpu.make_async_copy(xin.at[u, me], xin.at[u, me], local.at[u]).wait()
-            remote(u, xin.at[u, others]).wait_recv()
+            remote(u, xin.at[u]).wait_recv()
 
         @pl.when((half_index == 0) & (seg == 0))
         def _():
@@ -428,7 +431,7 @@
             prior[...] = cur[order[n - 1], half - 16 :, :].astype(f32)[8:]
 
         cur[...] = xin[u]
-        row_shift = lax.rem(8 - lax.rem(me * heads, 8) - g * hpg + 8, 8)
+        row_shift = lax.rem(8 - g * hpg, 8)
 
         def batch(first):
             blocks(
@@ -473,7 +476,7 @@
         def _():
             inc_ref[h] = jnp.zeros((HEAD_DIM, HEAD_DIM), f32)
 
-        @pl.when(seg == final)
+        @pl.when((seg == final) & (seg > 0))
         def _():
             with scope("hoplast"):
                 hop(h).wait_recv()
@@ -485,7 +488,7 @@
                 give(h, d - 1)
         block(h, me, state)
         give(h, n - 1)
-        pltpu.make_async_copy(y_ref.at[h, me], target(h, me), lout.at[1]).start()
+        pltpu.make_async_copy(y_ref.at[h, me], target(h, me), rsem.at[AT_Y]).start()
 
     for h in range(heads):
         g = h // hpg
@@ -495,19 +498,16 @@
                 with scope("forward"):
                     pl.when(jnp.minimum(seg, late) == turn)(lambda: forward(keys - 1))
         if h % hpg == 0:
-            pltpu.make_async_copy(oz[g].at[me], oz[g].at[me], local.at[units + 1 + g]).wait()
             with scope("zwait"):
-                remote(AT_Z + g, oz[g].at[others]).wait_recv()
+                remote(AT_Z + g, oz[g]).wait_recv()
         with scope("close"):
             close(h)
 
     with scope("waity"):
-        pltpu.make_async_copy(y_ref.at[:, 0], y_ref.at[:, 0], lout.at[1]).wait()
-        remote(AT_Y, y_ref.at[:, others]).wait_recv()
+        remote(AT_Y, y_ref).wait_recv()
     with scope("drain"):
         remote(AT_GATE, gbuf.at[others]).wait_send()
-        for u in range(units):
-            remote(u, xin.at[u, others]).wait_send()
+        remote(0, xin.at[:, others]).wait_send()
         for g in range(keys):
             remote(AT_Z + g, oz[g].at[others]).wait_send()
         remote(AT_Y, y_ref.at[:, others]).wait_send()
@@ -515,10 +515,11 @@
         @pl.when(seg < final)
         def _():
             remote(AT_TABLE, ptab).wait_send()
-            for g in range(keys):
-                remote(AT_TAIL + g, otail.at[g]).wait_send()
-            for h in range(heads):
-                hop(h).wait_send()
+            remote(AT_TAIL, otail).wait_send()
+            pltpu.make_async_remote_copy(
+                src_ref=pass_ref, dst_ref=inc_ref, send_sem=hsend, recv_sem=hrecv.at[0],
+                device_id=(after, me), device_id_type=MESH,
+            ).wait_send()
 
 
 def mixer(n, segs, heads, table, a_log, dt_bias, qkv, z, gates, conv_weight, gain):
@@ -545,11 +546,12 @@
             pltpu.VMEM(gain.shape, f32),
             pltpu.VMEM((half, qkv.shape[1]), bf16),
             pltpu.VMEM(gates.shape, bf16),
+            pltpu.VMEM((n, 8, BLOCK), bf16),
             pltpu.VMEM((TAIL, qkv.shape[1]), bf16),
             pltpu.VMEM((keys, n, TAIL, packed), bf16),
             pltpu.VMEM((units, n, half, wide), bf16),
             pltpu.VMEM((keys, n, TAIL, packed), bf16),
-            pltpu.VMEM((n, 2, 8, BLOCK), bf16),
+            pltpu.VMEM((n, 8, BLOCK), bf16),
             pltpu.VMEM(table.shape, jnp.int32),
             pltpu.VMEM((n, half, wide), bf16),
             pltpu.VMEM((TAIL, wide), f32),
@@ -565,11 +567,10 @@
             pltpu.VMEM((heads,) + square, f32),
             pltpu.VMEM((heads, n) + square, bf16),
             DMA((7,)),
-            DMA((units + 1 + keys,)),
-            DMA((2,)),
+            DMA,
+            DMA((kinds - units - keys + 2,)),
             DMA((kinds,)),
-            DMA((kinds,)),
-            DMA((heads,)),
+            DMA,
             DMA((heads,)),
             pltpu.SemaphoreType.REGULAR,
         ]

time: 52.2 us -> 52 us (level)
  no operation moved by 1% of the time
where the time goes in v3:
time: 52 us; the launch traced here: 51.3 us
  Pallas kernels  50.3 us (97%)
  local copies, waits for them, and re-layouts  0.97 us (2%)
    pallas_call x1, Pallas kernels, mixer(): pl.pallas_call(functools.partial(whole_kernel, n, segs, heads), out_shape...  50.3 us

profile of v3, /device:TPU:17, one launch (start us, length us, event | category | flops | bytes accessed | tf_op | source)
XLA Modules:
  0.0 51.3 jit_solution(8604481280237883222)
XLA Ops:
  0.0 50.3 %mixer.1 = bf16[128,4096]{1,0:T(8,128)(2,1)S(1)} custom-call(s32[1,16]{1,0:T(1,128)} %table_any.1, f32[32]{0:T(128)} %a_log_any.1, f32[32]{0:T(128)} %dt_bias_any.1, bf16[128,8192]{1,0:T(8,128)(2,1)} %qkv.1, bf16[128,4096]{1,0:T(8,128)(2,1)} %z.1, bf16[64,128]{1,0:T(8,128)(2,1)} %bitcast.2, f32[4,8192]{1,0:T(4,128)} %conv_weight.1, f32[1,128]{1,0:T(1,128)} %bitcast.3), custom_call_target="tpu_custom_call" | custom-call | tf_op jit(solution)/shard_map/mixer/pallas_call | solution.py:537
  50.3 1.0 %copy.10 = bf16[128,4096]{1,0:T(8,128)(2,1)} copy(bf16[128,4096]{1,0:T(8,128)(2,1)S(1)} %mixer.1) | data formatting | bytes 2097152

commit v4 on v3

--- a/solution.py
+++ b/solution.py
@@ -330,21 +330,6 @@
                 both = jnp.where(upper, pltpu.roll(tiles[i], TAIL // 2, 0), low)
                 tsend[g, p, :, i * HEAD_DIM : (i + 1) * HEAD_DIM] = both.astype(bf16)
 
-    @pl.when(seg < final)
-    def _():
-        with scope("readywait"):
-            pl.semaphore_wait(ready, 1)
-        post(AT_TABLE, table_any, ptab, (after, me))
-        for g in range(keys):
-            for d in range(n):
-                peer = lax.rem(me + d, n)
-                post(AT_TAIL + g, tsend.at[g, peer], otail.at[g, me], (after, peer))
-
-    for u in range(1, units):
-        post_all(u, lambda p: unit_pieces(p, u, me))
-    for g in range(keys):
-        post_all(AT_Z + g, lambda p: z_pieces(p, g, me))
-
     def find(b, carry):
         parity = lax.div(b, n)
         place = jnp.int32(0)
@@ -367,6 +352,21 @@
             st_ref[g, e, :, HEAD_DIM:] = jnp.where(row == col, 1.0, 0.0).astype(f32)
         rate_ref[g, 0] = -jnp.exp(scale)
         rate_ref[g, 1] = shift
+
+    @pl.when(seg < final)
+    def _():
+        with scope("readywait"):
+            pl.semaphore_wait(ready, 1)
+        post(AT_TABLE, table_any, ptab, (after, me))
+        for g in range(keys):
+            for d in range(n):
+                peer = lax.rem(me + d, n)
+                post(AT_TAIL + g, tsend.at[g, peer], otail.at[g, me], (after, peer))
+
+    for u in range(1, units):
+        post_all(u, lambda p: unit_pieces(p, u, me))
+    for g in range(keys):
+        post_all(AT_Z + g, lambda p: z_pieces(p, g, me))
 
     pltpu.make_async_copy(w_ref, w_ref, lout).wait()
     with scope("gatewait"):

time: 52 us -> 52 us (level)
  no operation moved by 1% of the time
where the time goes in v4:
time: 52 us; the launch traced here: 51.3 us
  Pallas kernels  50.3 us (97%)
  local copies, waits for them, and re-layouts  0.97 us (2%)
    pallas_call x1, Pallas kernels, mixer(): pl.pallas_call(functools.partial(whole_kernel, n, segs, heads), out_shape...  50.3 us

profile of v4, /device:TPU:17, one launch (start us, length us, event | category | flops | bytes accessed | tf_op | source)
XLA Modules:
  0.0 51.3 jit_solution(46431978865595179)
XLA Ops:
  0.0 50.3 %mixer.1 = bf16[128,4096]{1,0:T(8,128)(2,1)S(1)} custom-call(s32[1,16]{1,0:T(1,128)} %table_any.1, f32[32]{0:T(128)} %a_log_any.1, f32[32]{0:T(128)} %dt_bias_any.1, bf16[128,8192]{1,0:T(8,128)(2,1)} %qkv.1, bf16[128,4096]{1,0:T(8,128)(2,1)} %z.1, bf16[64,128]{1,0:T(8,128)(2,1)} %bitcast.2, f32[4,8192]{1,0:T(4,128)} %conv_weight.1, f32[1,128]{1,0:T(1,128)} %bitcast.3), custom_call_target="tpu_custom_call" | custom-call | tf_op jit(solution)/shard_map/mixer/pallas_call | solution.py:537
  50.3 1.0 %copy.10 = bf16[128,4096]{1,0:T(8,128)(2,1)} copy(bf16[128,4096]{1,0:T(8,128)(2,1)S(1)} %mixer.1) | data formatting | bytes 2097152

commit v5 on v4

--- a/solution.py
+++ b/solution.py
@@ -226,7 +226,6 @@
         for i, (src, dst) in enumerate(
             (
                 (gates, gstage),
-                (qkv.at[pl.ds(0, half)], stage),
                 (qkv.at[pl.ds(rows - TAIL, TAIL)], tstage),
                 (table_any, table),
                 (a_log_any, a_log),
@@ -235,6 +234,11 @@
             )
         )
     ]
+    firsts = sorted({p * heads // GROUP for p in range(n)})
+    ahead = [(i * HEAD_DIM, HEAD_DIM) for key in firsts for i in (key, KEY_HEADS + key)]
+    ahead += [((2 * KEY_HEADS + p * heads) * HEAD_DIM, wz) for p in range(n)]
+    for start, size in ahead:
+        pltpu.make_async_copy(qkv.at[pl.ds(0, half), pl.ds(start, size)], stage.at[:, pl.ds(start, size)], lin.at[6]).start()
     for copy in small:
         copy.start()
 
@@ -251,9 +255,9 @@
         )
 
     def unit_pieces(p, u, slot):
-        if u % 2 == 0:
+        if u == 0:
             return [(stage.at[:, src], xin.at[u, slot, :, dst]) for src, dst in places(p, u // 2)]
-        return [(qkv.at[pl.ds(half, half), src], xin.at[u, slot, :, dst]) for src, dst in places(p, u // 2)]
+        return [(qkv.at[pl.ds(u % 2 * half, half), src], xin.at[u, slot, :, dst]) for src, dst in places(p, u // 2)]
 
     def gate_pieces(p, slot):
         return [(gsend.at[p], gbuf.at[slot])]
@@ -274,7 +278,8 @@
         decay = pltpu.roll(gstage[VALUE_HEADS + tile : VALUE_HEADS + tile + 8].astype(f32), (12 - shift) % 8, 0)
         gsend[p] = jnp.where(line < 4, strength, decay).astype(bf16)
     gbuf[me] = gsend[me]
-    small[1].wait()
+    staged = stage.at[:, pl.ds(0, sum(size for _, size in ahead))]
+    pltpu.make_async_copy(staged, staged, lin.at[6]).wait()
     for kind, found in [(u, unit_pieces(me, u, me)) for u in range(units)] + [
         (AT_Z + g, z_pieces(me, g, me)) for g in range(keys)
     ]:
@@ -314,7 +319,7 @@
 
     post_all(AT_GATE, lambda p: gate_pieces(p, me))
     post_all(0, lambda p: unit_pieces(p, 0, me))
-    for copy in small[2:]:
+    for copy in small[1:]:
         copy.wait()
 
     wide = hpg + 2

time: 52 us -> 51.9 us (level)
  no operation moved by 1% of the time
where the time goes in v5:
time: 51.9 us; the launch traced here: 51.3 us
  Pallas kernels  50.3 us (97%)
  local copies, waits for them, and re-layouts  0.97 us (2%)
    pallas_call x1, Pallas kernels, mixer(): pl.pallas_call(functools.partial(whole_kernel, n, segs, heads), out_shape...  50.3 us

profile of v5, /device:TPU:17, one launch (start us, length us, event | category | flops | bytes accessed | tf_op | source)
XLA Modules:
  0.0 51.3 jit_solution(9712831711839778556)
XLA Ops:
  0.0 50.3 %mixer.1 = bf16[128,4096]{1,0:T(8,128)(2,1)S(1)} custom-call(s32[1,16]{1,0:T(1,128)} %table_any.1, f32[32]{0:T(128)} %a_log_any.1, f32[32]{0:T(128)} %dt_bias_any.1, bf16[128,8192]{1,0:T(8,128)(2,1)} %qkv.1, bf16[128,4096]{1,0:T(8,128)(2,1)} %z.1, bf16[64,128]{1,0:T(8,128)(2,1)} %bitcast.2, f32[4,8192]{1,0:T(4,128)} %conv_weight.1, f32[1,128]{1,0:T(1,128)} %bitcast.3), custom_call_target="tpu_custom_call" | custom-call | tf_op jit(solution)/shard_map/mixer/pallas_call | solution.py:542
  50.3 1.0 %copy.10 = bf16[128,4096]{1,0:T(8,128)(2,1)} copy(bf16[128,4096]{1,0:T(8,128)(2,1)S(1)} %mixer.1) | data formatting | bytes 2097152

commit v6 on v5

--- a/solution.py
+++ b/solution.py
@@ -358,17 +358,21 @@
         rate_ref[g, 0] = -jnp.exp(scale)
         rate_ref[g, 1] = shift
 
+    def post_tails(g):
+        for d in range(n):
+            peer = lax.rem(me + d, n)
+            post(AT_TAIL + g, tsend.at[g, peer], otail.at[g, me], (after, peer))
+
     @pl.when(seg < final)
     def _():
         with scope("readywait"):
             pl.semaphore_wait(ready, 1)
         post(AT_TABLE, table_any, ptab, (after, me))
-        for g in range(keys):
-            for d in range(n):
-                peer = lax.rem(me + d, n)
-                post(AT_TAIL + g, tsend.at[g, peer], otail.at[g, me], (after, peer))
+        post_tails(0)
 
     for u in range(1, units):
+        if u % 2 == 0:
+            pl.when(seg < final)(functools.partial(post_tails, u // 2))
         post_all(u, lambda p: unit_pieces(p, u, me))
     for g in range(keys):
         post_all(AT_Z + g, lambda p: z_pieces(p, g, me))

time: 51.9 us -> 51.9 us (level)
  no operation moved by 1% of the time
where the time goes in v6:
time: 51.9 us; the launch traced here: 51.3 us
  Pallas kernels  50.3 us (97%)
  local copies, waits for them, and re-layouts  0.97 us (2%)
    pallas_call x1, Pallas kernels, mixer(): pl.pallas_call(functools.partial(whole_kernel, n, segs, heads), out_shape...  50.3 us

profile of v6, /device:TPU:17, one launch (start us, length us, event | category | flops | bytes accessed | tf_op | source)
XLA Modules:
  0.0 51.3 jit_solution(6943736185101540187)
XLA Ops:
  0.0 50.3 %mixer.1 = bf16[128,4096]{1,0:T(8,128)(2,1)S(1)} custom-call(s32[1,16]{1,0:T(1,128)} %table_any.1, f32[32]{0:T(128)} %a_log_any.1, f32[32]{0:T(128)} %dt_bias_any.1, bf16[128,8192]{1,0:T(8,128)(2,1)} %qkv.1, bf16[128,4096]{1,0:T(8,128)(2,1)} %z.1, bf16[64,128]{1,0:T(8,128)(2,1)} %bitcast.2, f32[4,8192]{1,0:T(4,128)} %conv_weight.1, f32[1,128]{1,0:T(1,128)} %bitcast.3), custom_call_target="tpu_custom_call" | custom-call | tf_op jit(solution)/shard_map/mixer/pallas_call | solution.py:546
  50.3 1.0 %copy.10 = bf16[128,4096]{1,0:T(8,128)(2,1)} copy(bf16[128,4096]{1,0:T(8,128)(2,1)S(1)} %mixer.1) | data formatting | bytes 2097152
